TPU v7x, 32 devices: a whole 2x2x4 slice. The times are simulated.
32 devices in a mesh: sfc: 8 (over z, y), sub: 4 (over x, core).
Axes of the slice: x: 2, y: 2, z: 4, core: 2. Of those that a mesh axis runs over, the one named last changes fastest.
Arguments:
- vectors: float32 [64, 512, 256], P(None, ('sfc', 'sub')), may hold values from -10 to 10
- reaction: float32 [512, 256], P(('sfc', 'sub')), may hold values from 0.5 to 5
Outputs:
- basis: float32 [64, 512, 256], P(None, ('sfc', 'sub'))
- upper: float32 [64, 64], replicated
All inputs are finite; a program needn't handle non-finite values.
Results may differ from a plain program's by a relative error of at most 0.0003.
Values sent between devices are 32-bit elements; how exact they have to be, the bound alone decides.
A program may use at most 64 MiB of HBM per device.

v0:
```python
import math
import jax
import jax.numpy as jnp
from jax import lax
from jax.sharding import PartitionSpec as P

NY = 32
NL = 8
POWERS = 3
DELTA_MASS = 0.5


def with_halo(cells, sides, width):
    for axis, dim in sides:
        count = lax.axis_size(axis)
        ends = count - 1
        head = lax.slice_in_dim(cells, 0, width, axis=dim)
        tail = lax.slice_in_dim(cells, cells.shape[dim] - width, cells.shape[dim], axis=dim)
        cells = jnp.concatenate(
            [
                lax.ppermute(tail, axis, [(i, (i + 1) % count) for i in range(ends)]),
                cells,
                lax.ppermute(head, axis, [((i + 1) % count, i) for i in range(ends)]),
            ],
            axis=dim,
        )
    return cells


def line_tables(count):
    index = jnp.arange(count)
    offset = index[:, None] - index[None, :]
    near = (jnp.abs(offset) == 1).astype(jnp.float32)
    same = (offset == 0).astype(jnp.float32)
    mass = (4.0 * same + near) / 6.0
    stiff = 2.0 * same - near
    return (mass, stiff)


def tables(across, layers):
    mass_across, stiff_across = line_tables(across)
    mass_layers, stiff_layers = line_tables(layers)
    mass_plane = jnp.kron(mass_layers, mass_across)
    stiff_plane = (
        jnp.kron(mass_layers, stiff_across)
        + jnp.kron(stiff_layers, mass_across)
        + DELTA_MASS * mass_plane
    )
    return jnp.concatenate([mass_plane, stiff_plane], axis=1)


def plane_products(field, table):
    plane = table.shape[0]
    both = jnp.einsum("kzp,pq->kzq", field, table, precision=lax.Precision.HIGHEST)
    return (both[..., :plane], both[..., plane:])


def operate(field, reaction, table):
    massed, mixed = plane_products(field, table)
    edge_term = mixed / 6.0 - massed
    padded = with_halo(edge_term, ((("sfc", "sub"), 1),), 1)
    neighbours = padded[:, :-2] + padded[:, 2:]
    return neighbours + 4.0 / 6.0 * mixed + 2.0 * massed + reaction[None] * field


def whole_factor(local):
    gram = jnp.dot(local, local.T, precision=lax.Precision.HIGHEST)
    total = lax.psum(gram, ("sfc", "sub"))
    return jnp.linalg.cholesky(total)


def lower_solve(lower, block):
    return lax.linalg.triangular_solve(lower, block, left_side=True, lower=True)


def per_device(vectors, reaction):
    table = tables(NY, NL)
    field = vectors
    for _ in range(POWERS):
        field = operate(field, reaction, table)
    local = field.reshape(field.shape[0], -1)
    lower_one = whole_factor(local)
    first = lower_solve(lower_one, local)
    lower_two = whole_factor(first)
    second = lower_solve(lower_two, first)
    scale = math.sqrt(lax.axis_size("sfc") * lax.axis_size("sub") * local.shape[1])
    upper = jnp.dot(lower_one, lower_two, precision=lax.Precision.HIGHEST).T / scale
    return ((second * scale).reshape(vectors.shape), upper)


def solution(mesh):
    placed = (P(None, ("sfc", "sub"), None), P(("sfc", "sub"), None))
    return jax.shard_map(
        per_device,
        mesh=mesh,
        in_specs=placed,
        out_specs=(P(None, ("sfc", "sub"), None), P()),
        check_vma=False,
    )
```

profile of v0, /device:TPU:0, one launch (start us, length us, event | category | flops | bytes accessed | tf_op | source)
XLA Modules:
  0.0 152.5 jit_solution(1561632378919360733)
XLA Ops:
  0.7 0.3 broadcast_multiply_fusion
  1.0 0.0 copy-start
  1.0 0.3 mul.143
  1.3 0.3 add.78
  1.6 0.5 copy-done
  2.2 2.3 %convolution_bitcast_fusion = f32[64,16,512]{2,0,1:T(8,128)S(1)} fusion(f32[64,16,256]{2,1,0:T(8,128)S(1)} %copy-done, f32[256,256]{1,0:T(8,128)S(1)} %multiply_add_fusion.1, f32[256,256]{1,0:T(8,128)S(1)} %mul.143), kind=kOutput, calls=%fused_computation.1 | convolution fusion | flops 1610743808 | bytes 3670016 | tf_op jit(solution)/shard_map/kzp,pq->kzq/dot_general | solution.py:54
  4.5 0.0 copy-start.1
  4.5 0.2 multiply_subtract_fusion.2
  4.7 2.4 %collective-permute-start = (f32[64,1,256]{2,0,1:T(8,128)S(1)}, f32[64,1,256]{2,0,1:T(8,128)S(1)}, u32[]{:S(2)}, u32[]{:S(2)}) collective-permute-start(f32[64,1,256]{2,0,1:T(8,128)S(1)} %get-tuple-element.8), channel_id=1, source_target_pairs={{0,1},{1,2},{2,3},{3,4},{4,5},{5,6},{6,7},{7,8},{8,9},{9,10},{10,1... | collective-permute-start | bytes 196616 | tf_op jit(solution)/shard_map/ppermute | solution.py:21
  7.1 1.3 collective-permute-start.1
  8.4 0.0 collective-permute-done
  8.4 3.9 %collective-permute-done.1 = f32[64,1,256]{2,0,1:T(8,128)S(1)} collective-permute-done((f32[64,1,256]{2,0,1:T(8,128)S(1)}, f32[64,1,256]{2,0,1:T(8,128)S(1)}, u32[]{:S(2)}, u32[]{:S(2)}) %collective-permute-start.1) | collective-permute-done | bytes 65568 | tf_op jit(solution)/shard_map/ppermute | solution.py:23
  12.3 0.0 copy-done.1
  12.3 0.8 fusion.11
  13.2 1.8 %fusion.14 = f32[64,16,512]{2,0,1:T(8,128)S(1)} fusion(f32[64,16,256]{2,0,1:T(8,128)S(1)} %fusion.11, f32[256,256]{1,0:T(8,128)S(1)} %multiply_add_fusion.1, f32[256,256]{1,0:T(8,128)S(1)} %mul.143), kind=kOutput, calls=%fused_computation.30 | convolution fusion | flops 1610743808 | bytes 3670016 | tf_op jit(solution)/shard_map/kzp,pq->kzq/dot_general | solution.py:54
  15.0 0.2 multiply_subtract_fusion.1
  15.2 4.8 %collective-permute-start.2 = (f32[64,1,256]{2,0,1:T(8,128)S(1)}, f32[64,1,256]{2,0,1:T(8,128)S(1)}, u32[]{:S(2)}, u32[]{:S(2)}) collective-permute-start(f32[64,1,256]{2,0,1:T(8,128)S(1)} %get-tuple-element.6), channel_id=1, source_target_pairs={{0,1},{1,2},{2,3},{3,4},{4,5},{5,6},{6,7},{7,8},{8,9},{9,10},{10,1... | collective-permute-start | bytes 196616 | tf_op jit(solution)/shard_map/ppermute | solution.py:21
  20.0 1.3 collective-permute-start.3
  21.3 0.0 collective-permute-done.2
  21.4 1.8 %collective-permute-done.3 = f32[64,1,256]{2,0,1:T(8,128)S(1)} collective-permute-done((f32[64,1,256]{2,0,1:T(8,128)S(1)}, f32[64,1,256]{2,0,1:T(8,128)S(1)}, u32[]{:S(2)}, u32[]{:S(2)}) %collective-permute-start.3) | collective-permute-done | bytes 65568 | tf_op jit(solution)/shard_map/ppermute | solution.py:23
  23.2 0.3 fusion.7
  23.5 1.8 %fusion.13 = f32[64,16,512]{2,0,1:T(8,128)S(1)} fusion(f32[64,16,256]{2,0,1:T(8,128)S(1)} %fusion.7, f32[256,256]{1,0:T(8,128)S(1)} %multiply_add_fusion.1, f32[256,256]{1,0:T(8,128)S(1)} %mul.143), kind=kOutput, calls=%fused_computation.29 | convolution fusion | flops 1610743808 | bytes 3670016 | tf_op jit(solution)/shard_map/kzp,pq->kzq/dot_general | solution.py:54
  25.4 0.2 multiply_subtract_fusion
  25.6 5.1 %collective-permute-start.4 = (f32[64,1,256]{2,0,1:T(8,128)S(1)}, f32[64,1,256]{2,0,1:T(8,128)S(1)}, u32[]{:S(2)}, u32[]{:S(2)}) collective-permute-start(f32[64,1,256]{2,0,1:T(8,128)S(1)} %get-tuple-element.4), channel_id=1, source_target_pairs={{0,1},{1,2},{2,3},{3,4},{4,5},{5,6},{6,7},{7,8},{8,9},{9,10},{10,1... | collective-permute-start | bytes 196616 | tf_op jit(solution)/shard_map/ppermute | solution.py:21
  30.7 1.3 collective-permute-start.5
  32.0 0.0 collective-permute-done.4
  32.0 1.8 %collective-permute-done.5 = f32[64,1,256]{2,0,1:T(8,128)S(1)} collective-permute-done((f32[64,1,256]{2,0,1:T(8,128)S(1)}, f32[64,1,256]{2,0,1:T(8,128)S(1)}, u32[]{:S(2)}, u32[]{:S(2)}) %collective-permute-start.5) | collective-permute-done | bytes 65568 | tf_op jit(solution)/shard_map/ppermute | solution.py:23
  33.8 0.3 fusion.3
  34.1 1.0 convolution_bitcast_fusion.1
  35.1 45.9 %psum.14 = f32[64,64]{0,1:T(8,128)S(1)} all-reduce(f32[64,64]{0,1:T(8,128)S(1)} %convolution_bitcast_fusion.1), channel_id=1, replica_groups=mesh['sfc'=8,'sub'=4] {'sfc','sub'}, use_global_device_ids=true, to_apply=%region_0.1 | all-reduce | flops 4096 | bytes 32768 | tf_op jit(solution)/shard_map/psum | solution.py:68
  81.0 0.1 copy.25
  81.1 5.8 %cholesky.44 = f32[64,64]{1,0:T(8,128)S(1)} custom-call(f32[64,64]{1,0:T(8,128)S(1)} %fusion.19), custom_call_target="Cholesky" | custom-call | tf_op jit(solution)/shard_map/jit(cholesky)/cholesky | solution.py:69
  87.0 0.6 compare_reduce_fusion.1
  87.6 0.7 fusion.23
  88.3 4.9 %custom-call.6 = f32[1,64,64]{1,2,0:T(8,128)S(1)} custom-call(f32[1,64,64]{2,1,0:T(8,128)S(1)} %fusion.23), custom_call_target="InvertDiagBlocksLowerTriangular" | custom-call | tf_op jit(solution)/shard_map/triangular_solve/custom-call.0 | solution.py:73
  93.2 0.1 copy.36
  93.3 1.0 fusion.17
  94.3 1.0 fusion.44
  95.3 40.3 %psum.15 = f32[64,64]{0,1:T(8,128)S(1)} all-reduce(f32[64,64]{0,1:T(8,128)S(1)} %fusion.44), channel_id=1, replica_groups=mesh['sfc'=8,'sub'=4] {'sfc','sub'}, use_global_device_ids=true, to_apply=%region_3.6 | all-reduce | flops 4096 | bytes 32768 | tf_op jit(solution)/shard_map/psum | solution.py:68
  135.6 0.1 copy.28
  135.7 5.8 %cholesky.55 = f32[64,64]{1,0:T(8,128)S(1)} custom-call(f32[64,64]{1,0:T(8,128)S(1)} %fusion.16), custom_call_target="Cholesky" | custom-call | tf_op jit(solution)/shard_map/jit(cholesky)/cholesky | solution.py:69
  141.6 0.7 compare_reduce_fusion
  142.3 2.2 %convolution_multiply_fusion.1 = f32[64,64]{1,0:T(8,128)} fusion(f32[64,64]{1,0:T(8,128)S(1)} %cholesky.55, f32[64,64]{1,0:T(8,128)S(1)} %cholesky.44, pred[]{:T(512)} %compare_reduce_fusion, pred[]{:T(512)} %compare_reduce_fusion.1), kind=kOutput, calls=%fused_computation.2 | convolution fusion | flops 3174400 | bytes 49154 | tf_op jit(solution)/shard_map/dot_general | solution.py:87
  144.5 0.7 select_bitcast_fusion
  145.2 4.9 %custom-call.7 = f32[1,64,64]{1,2,0:T(8,128)S(1)} custom-call(f32[1,64,64]{2,1,0:T(8,128)S(1)} %select_bitcast_fusion), custom_call_target="InvertDiagBlocksLowerTriangular" | custom-call | tf_op jit(solution)/shard_map/triangular_solve/custom-call.0 | solution.py:73
  150.1 1.1 convolution_multiply_fusion
  151.2 1.3 copy.37
  (10 shorter events, 0.2 us)
Async XLA Ops:
  1.0 1.2 copy-start
  4.5 7.8 %copy-start.1 = (f32[16,256]{1,0:T(8,128)S(1)}, f32[16,256]{1,0:T(8,128)}, u32[]{:S(2)}) copy-start(f32[16,256]{1,0:T(8,128)} %param.6) | copy-start | bytes 49156
  4.7 3.7 %collective-permute-start = (f32[64,1,256]{2,0,1:T(8,128)S(1)}, f32[64,1,256]{2,0,1:T(8,128)S(1)}, u32[]{:S(2)}, u32[]{:S(2)}) collective-permute-start(f32[64,1,256]{2,0,1:T(8,128)S(1)} %get-tuple-element.8), channel_id=1, source_target_pairs={{0,1},{1,2},{2,3},{3,4},{4,5},{5,6},{6,7},{7,8},{8,9},{9,10},{10,1... | collective-permute-start | bytes 196616 | tf_op jit(solution)/shard_map/ppermute | solution.py:21
  7.1 5.2 %collective-permute-start.1 = (f32[64,1,256]{2,0,1:T(8,128)S(1)}, f32[64,1,256]{2,0,1:T(8,128)S(1)}, u32[]{:S(2)}, u32[]{:S(2)}) collective-permute-start(f32[64,1,256]{2,0,1:T(8,128)S(1)} %get-tuple-element.9), channel_id=1, source_target_pairs={{1,0},{2,1},{3,2},{4,3},{5,4},{6,5},{7,6},{8,7},{9,8},{10,9},{11,1... | collective-permute-start | bytes 196616 | tf_op jit(solution)/shard_map/ppermute | solution.py:23
  15.2 6.2 %collective-permute-start.2 = (f32[64,1,256]{2,0,1:T(8,128)S(1)}, f32[64,1,256]{2,0,1:T(8,128)S(1)}, u32[]{:S(2)}, u32[]{:S(2)}) collective-permute-start(f32[64,1,256]{2,0,1:T(8,128)S(1)} %get-tuple-element.6), channel_id=1, source_target_pairs={{0,1},{1,2},{2,3},{3,4},{4,5},{5,6},{6,7},{7,8},{8,9},{9,10},{10,1... | collective-permute-start | bytes 196616 | tf_op jit(solution)/shard_map/ppermute | solution.py:21
  20.0 3.1 %collective-permute-start.3 = (f32[64,1,256]{2,0,1:T(8,128)S(1)}, f32[64,1,256]{2,0,1:T(8,128)S(1)}, u32[]{:S(2)}, u32[]{:S(2)}) collective-permute-start(f32[64,1,256]{2,0,1:T(8,128)S(1)} %get-tuple-element.7), channel_id=1, source_target_pairs={{1,0},{2,1},{3,2},{4,3},{5,4},{6,5},{7,6},{8,7},{9,8},{10,9},{11,1... | collective-permute-start | bytes 196616 | tf_op jit(solution)/shard_map/ppermute | solution.py:23
  25.6 6.4 %collective-permute-start.4 = (f32[64,1,256]{2,0,1:T(8,128)S(1)}, f32[64,1,256]{2,0,1:T(8,128)S(1)}, u32[]{:S(2)}, u32[]{:S(2)}) collective-permute-start(f32[64,1,256]{2,0,1:T(8,128)S(1)} %get-tuple-element.4), channel_id=1, source_target_pairs={{0,1},{1,2},{2,3},{3,4},{4,5},{5,6},{6,7},{7,8},{8,9},{9,10},{10,1... | collective-permute-start | bytes 196616 | tf_op jit(solution)/shard_map/ppermute | solution.py:21
  30.7 3.1 %collective-permute-start.5 = (f32[64,1,256]{2,0,1:T(8,128)S(1)}, f32[64,1,256]{2,0,1:T(8,128)S(1)}, u32[]{:S(2)}, u32[]{:S(2)}) collective-permute-start(f32[64,1,256]{2,0,1:T(8,128)S(1)} %get-tuple-element.5), channel_id=1, source_target_pairs={{1,0},{2,1},{3,2},{4,3},{5,4},{6,5},{7,6},{8,7},{9,8},{10,9},{11,1... | collective-permute-start | bytes 196616 | tf_op jit(solution)/shard_map/ppermute | solution.py:23
where the time goes:
time: 153 us; the launch traced here: 152 us
  blocking collectives  86.2 us (56%)
  other arithmetic  26.6 us (17%)
  starting transfers between devices  16.2 us (11%)
  matrix products  12.2 us (8%)
  waiting for transfers between devices  7.62 us (5%)
  local copies, waits for them, and re-layouts  2.74 us (2%)
    psum x2, blocking collectives, whole_factor(): total = lax.psum(gram, ('sfc', 'sub'))  86.2 us
    another operation x6, other arithmetic, whole_factor(): return jnp.linalg.cholesky(total)  13.1 us
    ppermute x3, starting transfers between devices, with_halo(): lax.ppermute(tail, axis, [(i, (i + 1) % count) for i in range(ends)])  12.4 us
    another operation x4, other arithmetic, lower_solve(): return lax.linalg.triangular_solve(lower, block, left_side=True, lower=True)  11.1 us
    ppermute x3, waiting for transfers between devices, with_halo(): lax.ppermute(head, axis, [((i + 1) % count, i) for i in range(ends)])  7.61 us
    dot_general x3, matrix products, plane_products(): jnp.einsum('kzp,pq->kzq', field, table, precision=lax.Precision.HIGHEST)  5.98 us
    ppermute x3, starting transfers between devices, with_halo(): lax.ppermute(head, axis, [((i + 1) % count, i) for i in range(ends)])  3.88 us
  transfers between devices with their start and end apart: 6, of which 3 were waited for; matrix products, arithmetic and copies ran while one was open for 0% of the time, Pallas kernels for 0%

commit v1 on v0

--- a/solution.py
+++ b/solution.py
@@ -65,7 +65,7 @@
 
 def whole_factor(local):
     gram = jnp.dot(local, local.T, precision=lax.Precision.HIGHEST)
-    total = lax.psum(gram, ("sfc", "sub"))
+    total = lax.psum(lax.psum(gram, "sfc"), "sub")
     return jnp.linalg.cholesky(total)
 
 

time: 153 us -> 161 us (1.052)
  blocking collectives: 86.2 us -> 93.9 us
    psum x2 -> x4, blocking collectives: 86.2 us -> 93.9 us  [whole_factor(): total = lax.psum(lax.psum(gram, 'sfc'), 'sub')]
where the time goes in v1:
time: 161 us; the launch traced here: 160 us
  blocking collectives  93.9 us (58%)
  other arithmetic  26.6 us (17%)
  starting transfers between devices  16.2 us (10%)
  matrix products  12.2 us (8%)
  waiting for transfers between devices  7.62 us (5%)
  local copies, waits for them, and re-layouts  2.74 us (2%)
    psum x4, blocking collectives, whole_factor(): total = lax.psum(lax.psum(gram, 'sfc'), 'sub')  93.9 us
    another operation x6, other arithmetic, whole_factor(): return jnp.linalg.cholesky(total)  13.1 us
    ppermute x3, starting transfers between devices, with_halo(): lax.ppermute(tail, axis, [(i, (i + 1) % count) for i in range(ends)])  12.4 us
    another operation x4, other arithmetic, lower_solve(): return lax.linalg.triangular_solve(lower, block, left_side=True, lower=True)  11.1 us
    ppermute x3, waiting for transfers between devices, with_halo(): lax.ppermute(head, axis, [((i + 1) % count, i) for i in range(ends)])  7.61 us
    dot_general x3, matrix products, plane_products(): jnp.einsum('kzp,pq->kzq', field, table, precision=lax.Precision.HIGHEST)  5.98 us
    ppermute x3, starting transfers between devices, with_halo(): lax.ppermute(head, axis, [((i + 1) % count, i) for i in range(ends)])  3.88 us
  transfers between devices with their start and end apart: 6, of which 3 were waited for; matrix products, arithmetic and copies ran while one was open for 0% of the time, Pallas kernels for 0%

profile of v1, /device:TPU:0, one launch (start us, length us, event | category | flops | bytes accessed | tf_op | source)
XLA Modules:
  0.0 160.1 jit_solution(1731979829254288030)
XLA Ops:
  0.7 0.3 broadcast_multiply_fusion
  1.0 0.0 copy-start
  1.0 0.3 mul.143
  1.3 0.3 add.82
  1.6 0.5 copy-done
  2.2 2.3 %convolution_bitcast_fusion = f32[64,16,512]{2,0,1:T(8,128)S(1)} fusion(f32[64,16,256]{2,1,0:T(8,128)S(1)} %copy-done, f32[256,256]{1,0:T(8,128)S(1)} %multiply_add_fusion.1, f32[256,256]{1,0:T(8,128)S(1)} %mul.143), kind=kOutput, calls=%fused_computation.1 | convolution fusion | flops 1610743808 | bytes 3670016 | tf_op jit(solution)/shard_map/kzp,pq->kzq/dot_general | solution.py:54
  4.5 0.0 copy-start.1
  4.5 0.2 multiply_subtract_fusion.2
  4.7 2.4 %collective-permute-start = (f32[64,1,256]{2,0,1:T(8,128)S(1)}, f32[64,1,256]{2,0,1:T(8,128)S(1)}, u32[]{:S(2)}, u32[]{:S(2)}) collective-permute-start(f32[64,1,256]{2,0,1:T(8,128)S(1)} %get-tuple-element.8), channel_id=1, source_target_pairs={{0,1},{1,2},{2,3},{3,4},{4,5},{5,6},{6,7},{7,8},{8,9},{9,10},{10,1... | collective-permute-start | bytes 196616 | tf_op jit(solution)/shard_map/ppermute | solution.py:21
  7.1 1.3 collective-permute-start.1
  8.4 0.0 collective-permute-done
  8.4 3.9 %collective-permute-done.1 = f32[64,1,256]{2,0,1:T(8,128)S(1)} collective-permute-done((f32[64,1,256]{2,0,1:T(8,128)S(1)}, f32[64,1,256]{2,0,1:T(8,128)S(1)}, u32[]{:S(2)}, u32[]{:S(2)}) %collective-permute-start.1) | collective-permute-done | bytes 65568 | tf_op jit(solution)/shard_map/ppermute | solution.py:23
  12.3 0.8 fusion.11
  13.2 1.8 %fusion.14 = f32[64,16,512]{2,0,1:T(8,128)S(1)} fusion(f32[64,16,256]{2,0,1:T(8,128)S(1)} %fusion.11, f32[256,256]{1,0:T(8,128)S(1)} %multiply_add_fusion.1, f32[256,256]{1,0:T(8,128)S(1)} %mul.143), kind=kOutput, calls=%fused_computation.30 | convolution fusion | flops 1610743808 | bytes 3670016 | tf_op jit(solution)/shard_map/kzp,pq->kzq/dot_general | solution.py:54
  15.0 0.2 multiply_subtract_fusion.1
  15.2 4.8 %collective-permute-start.2 = (f32[64,1,256]{2,0,1:T(8,128)S(1)}, f32[64,1,256]{2,0,1:T(8,128)S(1)}, u32[]{:S(2)}, u32[]{:S(2)}) collective-permute-start(f32[64,1,256]{2,0,1:T(8,128)S(1)} %get-tuple-element.6), channel_id=1, source_target_pairs={{0,1},{1,2},{2,3},{3,4},{4,5},{5,6},{6,7},{7,8},{8,9},{9,10},{10,1... | collective-permute-start | bytes 196616 | tf_op jit(solution)/shard_map/ppermute | solution.py:21
  20.0 1.3 collective-permute-start.3
  21.3 0.0 collective-permute-done.2
  21.4 1.8 %collective-permute-done.3 = f32[64,1,256]{2,0,1:T(8,128)S(1)} collective-permute-done((f32[64,1,256]{2,0,1:T(8,128)S(1)}, f32[64,1,256]{2,0,1:T(8,128)S(1)}, u32[]{:S(2)}, u32[]{:S(2)}) %collective-permute-start.3) | collective-permute-done | bytes 65568 | tf_op jit(solution)/shard_map/ppermute | solution.py:23
  23.2 0.3 fusion.7
  23.5 1.8 %fusion.13 = f32[64,16,512]{2,0,1:T(8,128)S(1)} fusion(f32[64,16,256]{2,0,1:T(8,128)S(1)} %fusion.7, f32[256,256]{1,0:T(8,128)S(1)} %multiply_add_fusion.1, f32[256,256]{1,0:T(8,128)S(1)} %mul.143), kind=kOutput, calls=%fused_computation.29 | convolution fusion | flops 1610743808 | bytes 3670016 | tf_op jit(solution)/shard_map/kzp,pq->kzq/dot_general | solution.py:54
  25.4 0.2 multiply_subtract_fusion
  25.6 5.1 %collective-permute-start.4 = (f32[64,1,256]{2,0,1:T(8,128)S(1)}, f32[64,1,256]{2,0,1:T(8,128)S(1)}, u32[]{:S(2)}, u32[]{:S(2)}) collective-permute-start(f32[64,1,256]{2,0,1:T(8,128)S(1)} %get-tuple-element.4), channel_id=1, source_target_pairs={{0,1},{1,2},{2,3},{3,4},{4,5},{5,6},{6,7},{7,8},{8,9},{9,10},{10,1... | collective-permute-start | bytes 196616 | tf_op jit(solution)/shard_map/ppermute | solution.py:21
  30.7 1.3 collective-permute-start.5
  32.0 0.0 collective-permute-done.4
  32.0 1.8 %collective-permute-done.5 = f32[64,1,256]{2,0,1:T(8,128)S(1)} collective-permute-done((f32[64,1,256]{2,0,1:T(8,128)S(1)}, f32[64,1,256]{2,0,1:T(8,128)S(1)}, u32[]{:S(2)}, u32[]{:S(2)}) %collective-permute-start.5) | collective-permute-done | bytes 65568 | tf_op jit(solution)/shard_map/ppermute | solution.py:23
  33.8 0.3 fusion.3
  34.1 1.0 convolution_bitcast_fusion.1
  35.1 40.1 %psum.28 = f32[64,64]{0,1:T(8,128)S(1)} all-reduce(f32[64,64]{0,1:T(8,128)S(1)} %convolution_bitcast_fusion.1), channel_id=1, replica_groups=mesh['sfc'=8,'sub'=4] {'sfc'}, use_global_device_ids=true, to_apply=%region_0.1 | all-reduce | flops 4096 | bytes 32768 | tf_op jit(solution)/shard_map/psum | solution.py:68
  75.3 10.4 %psum.29 = f32[64,64]{0,1:T(8,128)S(1)} all-reduce(f32[64,64]{0,1:T(8,128)S(1)} %psum.28), channel_id=1, replica_groups=mesh['sfc'=8,'sub'=4] {'sub'}, use_global_device_ids=true, to_apply=%region_1.2 | all-reduce | flops 4096 | bytes 32768 | tf_op jit(solution)/shard_map/psum | solution.py:68
  85.7 0.1 copy.25
  85.8 5.8 %cholesky.44 = f32[64,64]{1,0:T(8,128)S(1)} custom-call(f32[64,64]{1,0:T(8,128)S(1)} %fusion.19), custom_call_target="Cholesky" | custom-call | tf_op jit(solution)/shard_map/jit(cholesky)/cholesky | solution.py:69
  91.7 0.6 compare_reduce_fusion.1
  92.3 0.7 fusion.23
  93.0 4.9 %custom-call.6 = f32[1,64,64]{1,2,0:T(8,128)S(1)} custom-call(f32[1,64,64]{2,1,0:T(8,128)S(1)} %fusion.23), custom_call_target="InvertDiagBlocksLowerTriangular" | custom-call | tf_op jit(solution)/shard_map/triangular_solve/custom-call.0 | solution.py:73
  97.9 0.1 copy.36
  98.0 1.0 fusion.17
  99.0 1.0 fusion.44
  100.0 33.0 %psum.30 = f32[64,64]{0,1:T(8,128)S(1)} all-reduce(f32[64,64]{0,1:T(8,128)S(1)} %fusion.44), channel_id=1, replica_groups=mesh['sfc'=8,'sub'=4] {'sfc'}, use_global_device_ids=true, to_apply=%region_4.7 | all-reduce | flops 4096 | bytes 32768 | tf_op jit(solution)/shard_map/psum | solution.py:68
  133.0 10.3 %psum.31 = f32[64,64]{0,1:T(8,128)S(1)} all-reduce(f32[64,64]{0,1:T(8,128)S(1)} %psum.30), channel_id=1, replica_groups=mesh['sfc'=8,'sub'=4] {'sub'}, use_global_device_ids=true, to_apply=%region_5.8 | all-reduce | flops 4096 | bytes 32768 | tf_op jit(solution)/shard_map/psum | solution.py:68
  143.3 0.1 copy.28
  143.4 5.8 %cholesky.55 = f32[64,64]{1,0:T(8,128)S(1)} custom-call(f32[64,64]{1,0:T(8,128)S(1)} %fusion.16), custom_call_target="Cholesky" | custom-call | tf_op jit(solution)/shard_map/jit(cholesky)/cholesky | solution.py:69
  149.3 0.7 compare_reduce_fusion
  150.0 2.2 %convolution_multiply_fusion.1 = f32[64,64]{1,0:T(8,128)} fusion(f32[64,64]{1,0:T(8,128)S(1)} %cholesky.55, f32[64,64]{1,0:T(8,128)S(1)} %cholesky.44, pred[]{:T(512)} %compare_reduce_fusion, pred[]{:T(512)} %compare_reduce_fusion.1), kind=kOutput, calls=%fused_computation.2 | convolution fusion | flops 3174400 | bytes 49154 | tf_op jit(solution)/shard_map/dot_general | solution.py:87
  152.2 0.7 select_bitcast_fusion
  152.9 4.9 %custom-call.7 = f32[1,64,64]{1,2,0:T(8,128)S(1)} custom-call(f32[1,64,64]{2,1,0:T(8,128)S(1)} %select_bitcast_fusion), custom_call_target="InvertDiagBlocksLowerTriangular" | custom-call | tf_op jit(solution)/shard_map/triangular_solve/custom-call.0 | solution.py:73
  157.8 1.1 convolution_multiply_fusion
  158.8 1.3 copy.37
  (11 shorter events, 0.2 us)
Async XLA Ops:
  1.0 1.2 copy-start
  4.5 7.8 %copy-start.1 = (f32[16,256]{1,0:T(8,128)S(1)}, f32[16,256]{1,0:T(8,128)}, u32[]{:S(2)}) copy-start(f32[16,256]{1,0:T(8,128)} %param.6) | copy-start | bytes 49156
  4.7 3.7 %collective-permute-start = (f32[64,1,256]{2,0,1:T(8,128)S(1)}, f32[64,1,256]{2,0,1:T(8,128)S(1)}, u32[]{:S(2)}, u32[]{:S(2)}) collective-permute-start(f32[64,1,256]{2,0,1:T(8,128)S(1)} %get-tuple-element.8), channel_id=1, source_target_pairs={{0,1},{1,2},{2,3},{3,4},{4,5},{5,6},{6,7},{7,8},{8,9},{9,10},{10,1... | collective-permute-start | bytes 196616 | tf_op jit(solution)/shard_map/ppermute | solution.py:21
  7.1 5.2 %collective-permute-start.1 = (f32[64,1,256]{2,0,1:T(8,128)S(1)}, f32[64,1,256]{2,0,1:T(8,128)S(1)}, u32[]{:S(2)}, u32[]{:S(2)}) collective-permute-start(f32[64,1,256]{2,0,1:T(8,128)S(1)} %get-tuple-element.9), channel_id=1, source_target_pairs={{1,0},{2,1},{3,2},{4,3},{5,4},{6,5},{7,6},{8,7},{9,8},{10,9},{11,1... | collective-permute-start | bytes 196616 | tf_op jit(solution)/shard_map/ppermute | solution.py:23
  15.2 6.2 %collective-permute-start.2 = (f32[64,1,256]{2,0,1:T(8,128)S(1)}, f32[64,1,256]{2,0,1:T(8,128)S(1)}, u32[]{:S(2)}, u32[]{:S(2)}) collective-permute-start(f32[64,1,256]{2,0,1:T(8,128)S(1)} %get-tuple-element.6), channel_id=1, source_target_pairs={{0,1},{1,2},{2,3},{3,4},{4,5},{5,6},{6,7},{7,8},{8,9},{9,10},{10,1... | collective-permute-start | bytes 196616 | tf_op jit(solution)/shard_map/ppermute | solution.py:21
  20.0 3.1 %collective-permute-start.3 = (f32[64,1,256]{2,0,1:T(8,128)S(1)}, f32[64,1,256]{2,0,1:T(8,128)S(1)}, u32[]{:S(2)}, u32[]{:S(2)}) collective-permute-start(f32[64,1,256]{2,0,1:T(8,128)S(1)} %get-tuple-element.7), channel_id=1, source_target_pairs={{1,0},{2,1},{3,2},{4,3},{5,4},{6,5},{7,6},{8,7},{9,8},{10,9},{11,1... | collective-permute-start | bytes 196616 | tf_op jit(solution)/shard_map/ppermute | solution.py:23
  25.6 6.4 %collective-permute-start.4 = (f32[64,1,256]{2,0,1:T(8,128)S(1)}, f32[64,1,256]{2,0,1:T(8,128)S(1)}, u32[]{:S(2)}, u32[]{:S(2)}) collective-permute-start(f32[64,1,256]{2,0,1:T(8,128)S(1)} %get-tuple-element.4), channel_id=1, source_target_pairs={{0,1},{1,2},{2,3},{3,4},{4,5},{5,6},{6,7},{7,8},{8,9},{9,10},{10,1... | collective-permute-start | bytes 196616 | tf_op jit(solution)/shard_map/ppermute | solution.py:21
  30.7 3.1 %collective-permute-start.5 = (f32[64,1,256]{2,0,1:T(8,128)S(1)}, f32[64,1,256]{2,0,1:T(8,128)S(1)}, u32[]{:S(2)}, u32[]{:S(2)}) collective-permute-start(f32[64,1,256]{2,0,1:T(8,128)S(1)} %get-tuple-element.5), channel_id=1, source_target_pairs={{1,0},{2,1},{3,2},{4,3},{5,4},{6,5},{7,6},{8,7},{9,8},{10,9},{11,1... | collective-permute-start | bytes 196616 | tf_op jit(solution)/shard_map/ppermute | solution.py:23
